TPU v7x, 32 devices: a whole 2x2x4 slice. The times are simulated.
32 devices in a mesh: dp: 8 (over y, x, core), fsdp: 4 (over z).
Axes of the slice: x: 2, y: 2, z: 4, core: 2. Of those that a mesh axis runs over, the one named last changes fastest.
Arguments:
- grads: float32 [32, 96, 128], P(('dp', 'fsdp')), may hold values from -0.6 to 0.6
- last_peak: float32 [96], replicated, may hold values from 0.05 to 0.8
- master: float32 [96, 128], P(('dp', 'fsdp')), may hold values from -6 to 6
- moment1: float32 [96, 128], P(('dp', 'fsdp')), may hold values from -6 to 6
- moment2: float32 [96, 128], P(('dp', 'fsdp')), may hold values from 0.25 to 8
Outputs:
- new_master: float32 [96, 128], P(('dp', 'fsdp'))
- new_moment1: float32 [96, 128], P(('dp', 'fsdp'))
- new_moment2: float32 [96, 128], P(('dp', 'fsdp'))
- weights: bfloat16 [96, 128], replicated
- block_peak: float32 [96], replicated
All inputs are finite; a program needn't handle non-finite values.
Results may differ from a plain program's by a relative error of at most 0.0035.
Values may be sent and summed in bfloat16 or wider, within the bound.
No kernel may reach another device: no remote copies, remote signals or barrier semaphores. Data moves between devices by JAX's collectives and lax.ppermute only.
A program may use at most 64 MiB of HBM per device.

v0:
```python
import jax
import jax.numpy as jnp
from jax import lax
from jax.sharding import PartitionSpec as P

STEP_COUNT = 10
code_limit = 448.0
peak_floor = 0.05
beta_one = 0.9
beta_two = 0.95
learn_rate = 0.05
decay_rate = 0.1
epsilon = 1e-08


def quantize(rows, inverse):
    codes = jnp.clip(rows * inverse[:, None], -code_limit, code_limit).astype(jnp.bfloat16)
    return lax.optimization_barrier(codes).astype(jnp.float32)


def adamw(gradient, master, moment1, moment2):
    first = beta_one * moment1 + (1.0 - beta_one) * gradient
    second = beta_two * moment2 + (1.0 - beta_two) * gradient * gradient
    corrected_one = first / (1.0 - beta_one**STEP_COUNT)
    corrected_two = second / (1.0 - beta_two**STEP_COUNT)
    updated = master - learn_rate * (
        corrected_one / (jnp.sqrt(corrected_two) + epsilon) + decay_rate * master
    )
    return (updated, first, second)


def body(grads, last_peak, master, moment1, moment2):
    local = grads[0]
    peak = lax.pmax(jnp.max(jnp.abs(local), axis=1), ("dp", "fsdp"))
    floored = jnp.maximum(last_peak, peak_floor)
    inverse = code_limit / floored
    scale = floored / code_limit
    owned = master.shape[0]
    first_row = lax.axis_index(("dp", "fsdp")) * owned
    summed = lax.psum_scatter(
        quantize(local, inverse), ("dp", "fsdp"), scatter_dimension=0, tiled=True
    )
    own_scale = lax.dynamic_slice_in_dim(scale, first_row, owned, 0)
    gradient = summed * own_scale[:, None]
    updated, first, second = adamw(gradient, master, moment1, moment2)
    rounded = updated.astype(jnp.bfloat16)
    grouped_rows = lax.all_gather(rounded, "fsdp", axis=0, tiled=True)
    weights = lax.all_gather(grouped_rows, "dp", axis=0, tiled=True)
    return (updated, first, second, weights, peak)


def solution(mesh):
    placed = (
        P(("dp", "fsdp"), None, None),
        P(),
        P(("dp", "fsdp"), None),
        P(("dp", "fsdp"), None),
        P(("dp", "fsdp"), None),
    )
    return jax.shard_map(
        body,
        mesh=mesh,
        in_specs=placed,
        out_specs=(
            P(("dp", "fsdp"), None),
            P(("dp", "fsdp"), None),
            P(("dp", "fsdp"), None),
            P(),
            P(),
        ),
        check_vma=False,
    )
```

profile of v0, /device:TPU:12, one launch (start us, length us, event | category | flops | bytes accessed | tf_op | source)
XLA Modules:
  0.0 103.9 jit_solution(240758746087156561)
XLA Ops:
  0.6 0.0 copy-start.3
  0.6 0.6 copy-done.3
  1.3 0.1 dynamic_slice.3
  1.4 1.0 fusion.2
  2.4 41.5 %all-reduce = f32[96,128]{1,0:T(8,128)S(1)} all-reduce(bf16[96,128]{1,0:T(8,128)(2,1)S(1)} %get-tuple-element.10), channel_id=2, replica_groups=mesh['dp'=8,'fsdp'=4] {'dp','fsdp'}, use_global_device_ids=true, to_apply=%region_0.0.clone | all-reduce | flops 12288 | bytes 73728
  43.9 0.0 copy-start.2
  43.9 0.0 copy-start
  43.9 0.0 copy-start.1
  43.9 0.6 copy-done.2
  44.6 0.0 copy-done
  44.6 0.0 copy-done.1
  44.6 0.7 convert_bitcast_fusion
  45.3 8.1 %all-gather = bf16[4,3,128]{2,1,0:T(4,128)(2,1)S(1)} all-gather(bf16[1,3,128]{2,1,0:T(4,128)(2,1)S(1)} %get-tuple-element.5), channel_id=1, replica_groups=mesh['dp'=8,'fsdp'=4] {'fsdp'}, dimensions={0}, use_global_device_ids=true | all-gather | bytes 3840 | tf_op jit(solution)/shard_map/all_gather | solution.py:47
  53.4 8.1 %all-gather.1 = bf16[8,12,128]{2,1,0:T(8,128)(2,1)S(1)} all-gather(bf16[1,12,128]{2,1,0:T(8,128)(2,1)S(1)} %reshape.14), channel_id=1, replica_groups=mesh['dp'=8,'fsdp'=4] {'dp'}, dimensions={0}, use_global_device_ids=true | all-gather | bytes 27648 | tf_op jit(solution)/shard_map/all_gather | solution.py:48
  61.5 0.6 reshape.15
  62.1 41.7 %pmax.7 = f32[96]{0:T(128)} all-reduce(f32[96]{0:T(128)S(1)} %get-tuple-element.9), channel_id=1, replica_groups=mesh['dp'=8,'fsdp'=4] {'dp','fsdp'}, use_global_device_ids=true, to_apply=%region_2.3 | all-reduce | flops 96 | bytes 768 | tf_op jit(solution)/shard_map/pmax | solution.py:34
  (2 shorter events, 0.0 us)
Async XLA Ops:
  0.6 0.7 copy-start.3
  43.9 0.7 copy-start.2
  43.9 0.7 copy-start
  43.9 0.7 copy-start.1
where the time goes:
time: 104 us
  blocking collectives  99.5 us (96%)
  local copies, waits for them, and re-layouts  2.05 us (2%)
  other arithmetic  1.66 us (2%)
    pmax x1, blocking collectives, body(): peak = lax.pmax(jnp.max(jnp.abs(local), axis=1), ('dp', 'fsdp'))  41.7 us
    unnamed x1, blocking collectives  41.5 us
    all_gather x1, blocking collectives, body(): weights = lax.all_gather(grouped_rows, 'dp', axis=0, tiled=True)  8.11 us
    all_gather x1, blocking collectives, body(): grouped_rows = lax.all_gather(rounded, 'fsdp', axis=0, tiled=True)  8.08 us

commit v1 on v0

--- a/solution.py
+++ b/solution.py
@@ -11,6 +11,20 @@
 learn_rate = 0.05
 decay_rate = 0.1
 epsilon = 1e-08
+
+
+def turn_grid(xx):
+    chunks = []
+    n_parts = lax.axis_size("dp")
+    for m in [*range(n_parts)]:
+        chunks.append((m, (m + 1) % n_parts))
+    local_part = [None] * n_parts
+    local_part[n_parts - 1] = xx
+    for idx in range(n_parts - 2, -1, -1):
+        local_part[idx] = lax.ppermute(local_part[idx + 1], axis_name="dp", perm=chunks)
+    u_next = jnp.concatenate(local_part, 0)
+    mixed_arr = (lax.axis_index("dp") + 1) * xx.shape[0]
+    return jnp.roll(u_next, mixed_arr, 0)
 
 
 def quantize(rows, inverse):
@@ -45,7 +59,7 @@
     updated, first, second = adamw(gradient, master, moment1, moment2)
     rounded = updated.astype(jnp.bfloat16)
     grouped_rows = lax.all_gather(rounded, "fsdp", axis=0, tiled=True)
-    weights = lax.all_gather(grouped_rows, "dp", axis=0, tiled=True)
+    weights = turn_grid(grouped_rows)
     return (updated, first, second, weights, peak)
 
 

time: 104 us -> 121 us (1.16)
  waiting for transfers between devices: 0 us -> 23.6 us
  blocking collectives: 99.5 us -> 91.4 us
    ppermute x0 -> x7, waiting for transfers between devices: none -> 23.6 us  [turn_grid(): lax.ppermute(local_part[idx + 1], axis_name='dp', perm=chunks)]
    all_gather x1 -> x0, blocking collectives: 8.11 us -> none  [body(): weights = lax.all_gather(grouped_rows, 'dp', axis=0, tiled=True)]
  transfers between devices with their start and end apart: 0 -> 7, of which waited for: 0 -> 6; matrix products, arithmetic and copies ran while one was open for 0% -> 0% of each run, Pallas kernels for 0% -> 0%
where the time goes in v1:
time: 121 us; the launch traced here: 120 us
  blocking collectives  91.4 us (76%)
  waiting for transfers between devices  23.6 us (20%)
  local copies, waits for them, and re-layouts  2.91 us (2%)
  other arithmetic  1.66 us (1%)
    pmax x1, blocking collectives, body(): peak = lax.pmax(jnp.max(jnp.abs(local), axis=1), ('dp', 'fsdp'))  41.8 us
    unnamed x1, blocking collectives  41.5 us
    ppermute x7, waiting for transfers between devices, turn_grid(): lax.ppermute(local_part[idx + 1], axis_name='dp', perm=chunks)  23.6 us
    all_gather x1, blocking collectives, body(): grouped_rows = lax.all_gather(rounded, 'fsdp', axis=0, tiled=True)  8.08 us
  transfers between devices with their start and end apart: 7, of which 6 were waited for; matrix products, arithmetic and copies ran while one was open for 0% of the time, Pallas kernels for 0%

profile of v1, /device:TPU:12, one launch (start us, length us, event | category | flops | bytes accessed | tf_op | source)
XLA Modules:
  0.0 120.3 jit_solution(10499193968160432412)
XLA Ops:
  0.6 0.0 copy-start.3
  0.7 0.6 copy-done.3
  1.3 1.0 fusion.2
  2.3 41.5 %all-reduce = f32[96,128]{1,0:T(8,128)S(1)} all-reduce(bf16[96,128]{1,0:T(8,128)(2,1)S(1)} %get-tuple-element.10), channel_id=2, replica_groups=mesh['dp'=8,'fsdp'=4] {'dp','fsdp'}, use_global_device_ids=true, to_apply=%region_0.0.clone | all-reduce | flops 12288 | bytes 73728
  43.8 0.0 copy-start.2
  43.8 0.0 copy-start.1
  43.9 0.0 copy-start
  43.9 0.1 dynamic_slice.7
  43.9 0.6 copy-done.2
  44.5 0.0 copy-done.1
  44.5 0.0 copy-done
  44.5 0.7 convert_bitcast_fusion
  45.2 8.1 %all-gather = bf16[4,3,128]{2,1,0:T(4,128)(2,1)S(1)} all-gather(bf16[1,3,128]{2,1,0:T(4,128)(2,1)S(1)} %get-tuple-element.5), channel_id=1, replica_groups=mesh['dp'=8,'fsdp'=4] {'fsdp'}, dimensions={0}, use_global_device_ids=true | all-gather | bytes 3840 | tf_op jit(solution)/shard_map/all_gather | solution.py:61
  53.3 0.0 collective-permute-start
  53.3 3.9 %collective-permute-done = bf16[12,128]{1,0:T(8,128)(2,1)S(1)} collective-permute-done((bf16[12,128]{1,0:T(8,128)(2,1)S(1)}, bf16[12,128]{1,0:T(8,128)(2,1)S(1)}, u32[]{:S(2)}, u32[]{:S(2)}) %collective-permute-start) | collective-permute-done | bytes 3104 | tf_op jit(solution)/shard_map/ppermute | solution.py:24
  57.2 0.0 collective-permute-start.1
  57.2 3.9 %collective-permute-done.1 = bf16[12,128]{1,0:T(8,128)(2,1)S(1)} collective-permute-done((bf16[12,128]{1,0:T(8,128)(2,1)S(1)}, bf16[12,128]{1,0:T(8,128)(2,1)S(1)}, u32[]{:S(2)}, u32[]{:S(2)}) %collective-permute-start.1) | collective-permute-done | bytes 3104 | tf_op jit(solution)/shard_map/ppermute | solution.py:24
  61.2 0.0 collective-permute-start.2
  61.2 3.9 %collective-permute-done.2 = bf16[12,128]{1,0:T(8,128)(2,1)S(1)} collective-permute-done((bf16[12,128]{1,0:T(8,128)(2,1)S(1)}, bf16[12,128]{1,0:T(8,128)(2,1)S(1)}, u32[]{:S(2)}, u32[]{:S(2)}) %collective-permute-start.2) | collective-permute-done | bytes 3104 | tf_op jit(solution)/shard_map/ppermute | solution.py:24
  65.1 0.0 collective-permute-start.3
  65.1 3.9 %collective-permute-done.3 = bf16[12,128]{1,0:T(8,128)(2,1)S(1)} collective-permute-done((bf16[12,128]{1,0:T(8,128)(2,1)S(1)}, bf16[12,128]{1,0:T(8,128)(2,1)S(1)}, u32[]{:S(2)}, u32[]{:S(2)}) %collective-permute-start.3) | collective-permute-done | bytes 3104 | tf_op jit(solution)/shard_map/ppermute | solution.py:24
  69.0 0.0 collective-permute-start.4
  69.0 3.9 %collective-permute-done.4 = bf16[12,128]{1,0:T(8,128)(2,1)S(1)} collective-permute-done((bf16[12,128]{1,0:T(8,128)(2,1)S(1)}, bf16[12,128]{1,0:T(8,128)(2,1)S(1)}, u32[]{:S(2)}, u32[]{:S(2)}) %collective-permute-start.4) | collective-permute-done | bytes 3104 | tf_op jit(solution)/shard_map/ppermute | solution.py:24
  73.0 0.0 collective-permute-start.5
  73.0 3.9 %collective-permute-done.5 = bf16[12,128]{1,0:T(8,128)(2,1)S(1)} collective-permute-done((bf16[12,128]{1,0:T(8,128)(2,1)S(1)}, bf16[12,128]{1,0:T(8,128)(2,1)S(1)}, u32[]{:S(2)}, u32[]{:S(2)}) %collective-permute-start.5) | collective-permute-done | bytes 3104 | tf_op jit(solution)/shard_map/ppermute | solution.py:24
  76.9 0.0 collective-permute-start.6
  76.9 41.8 %pmax.7 = f32[96]{0:T(128)} all-reduce(f32[96]{0:T(128)S(1)} %get-tuple-element.9), channel_id=1, replica_groups=mesh['dp'=8,'fsdp'=4] {'dp','fsdp'}, use_global_device_ids=true, to_apply=%region_2.3 | all-reduce | flops 96 | bytes 768 | tf_op jit(solution)/shard_map/pmax | solution.py:48
  118.7 0.0 collective-permute-done.6
  118.7 0.9 concatenate.6
  119.7 0.6 constant_dynamic-slice_fusion
  (2 shorter events, 0.0 us)
Async XLA Ops:
  0.6 0.7 copy-start.3
  43.8 0.7 copy-start.2
  43.8 0.7 copy-start.1
  43.9 0.7 copy-start
  53.3 3.9 %collective-permute-start = (bf16[12,128]{1,0:T(8,128)(2,1)S(1)}, bf16[12,128]{1,0:T(8,128)(2,1)S(1)}, u32[]{:S(2)}, u32[]{:S(2)}) collective-permute-start(bf16[12,128]{1,0:T(8,128)(2,1)S(1)} %reshape.13), channel_id=1, source_target_pairs={{0,4},{4,8},{8,12},{12,16},{16,20},{20,24},{24,28},{28,0},{1,5},{5... | collective-permute-start | bytes 9224 | tf_op jit(solution)/shard_map/ppermute | solution.py:24
  57.2 3.9 %collective-permute-start.1 = (bf16[12,128]{1,0:T(8,128)(2,1)S(1)}, bf16[12,128]{1,0:T(8,128)(2,1)S(1)}, u32[]{:S(2)}, u32[]{:S(2)}) collective-permute-start(bf16[12,128]{1,0:T(8,128)(2,1)S(1)} %collective-permute-done), channel_id=1, source_target_pairs={{0,4},{4,8},{8,12},{12,16},{16,20},{20,24},{24,28},{28,0},{1,5},{5... | collective-permute-start | bytes 9224 | tf_op jit(solution)/shard_map/ppermute | solution.py:24
  61.2 3.9 %collective-permute-start.2 = (bf16[12,128]{1,0:T(8,128)(2,1)S(1)}, bf16[12,128]{1,0:T(8,128)(2,1)S(1)}, u32[]{:S(2)}, u32[]{:S(2)}) collective-permute-start(bf16[12,128]{1,0:T(8,128)(2,1)S(1)} %collective-permute-done.1), channel_id=1, source_target_pairs={{0,4},{4,8},{8,12},{12,16},{16,20},{20,24},{24,28},{28,0},{1,5},{5... | collective-permute-start | bytes 9224 | tf_op jit(solution)/shard_map/ppermute | solution.py:24
  65.1 3.9 %collective-permute-start.3 = (bf16[12,128]{1,0:T(8,128)(2,1)S(1)}, bf16[12,128]{1,0:T(8,128)(2,1)S(1)}, u32[]{:S(2)}, u32[]{:S(2)}) collective-permute-start(bf16[12,128]{1,0:T(8,128)(2,1)S(1)} %collective-permute-done.2), channel_id=1, source_target_pairs={{0,4},{4,8},{8,12},{12,16},{16,20},{20,24},{24,28},{28,0},{1,5},{5... | collective-permute-start | bytes 9224 | tf_op jit(solution)/shard_map/ppermute | solution.py:24
  69.0 3.9 %collective-permute-start.4 = (bf16[12,128]{1,0:T(8,128)(2,1)S(1)}, bf16[12,128]{1,0:T(8,128)(2,1)S(1)}, u32[]{:S(2)}, u32[]{:S(2)}) collective-permute-start(bf16[12,128]{1,0:T(8,128)(2,1)S(1)} %collective-permute-done.3), channel_id=1, source_target_pairs={{0,4},{4,8},{8,12},{12,16},{16,20},{20,24},{24,28},{28,0},{1,5},{5... | collective-permute-start | bytes 9224 | tf_op jit(solution)/shard_map/ppermute | solution.py:24
  73.0 3.9 %collective-permute-start.5 = (bf16[12,128]{1,0:T(8,128)(2,1)S(1)}, bf16[12,128]{1,0:T(8,128)(2,1)S(1)}, u32[]{:S(2)}, u32[]{:S(2)}) collective-permute-start(bf16[12,128]{1,0:T(8,128)(2,1)S(1)} %collective-permute-done.4), channel_id=1, source_target_pairs={{0,4},{4,8},{8,12},{12,16},{16,20},{20,24},{24,28},{28,0},{1,5},{5... | collective-permute-start | bytes 9224 | tf_op jit(solution)/shard_map/ppermute | solution.py:24
  76.9 41.8 %collective-permute-start.6 = (bf16[12,128]{1,0:T(8,128)(2,1)S(1)}, bf16[12,128]{1,0:T(8,128)(2,1)S(1)}, u32[]{:S(2)}, u32[]{:S(2)}) collective-permute-start(bf16[12,128]{1,0:T(8,128)(2,1)S(1)} %collective-permute-done.5), channel_id=1, source_target_pairs={{0,4},{4,8},{8,12},{12,16},{16,20},{20,24},{24,28},{28,0},{1,5},{5... | collective-permute-start | bytes 9224 | tf_op jit(solution)/shard_map/ppermute | solution.py:24
